TPU v7x, 256 devices: a whole 4x4x8 slice. The times are simulated.
256 devices in a mesh: ulysses: 16 (over z, x_hi), blk: 16 (over y, x_lo, core).
Axes of the slice: x: 4 (x_hi: 2, x_lo: 2; x = x_hi * 2 + x_lo), y: 4, z: 8, core: 2. Of those that a mesh axis runs over, the one named last changes fastest.
Arguments:
- queries: bfloat16 [16, 1024, 4096], P('blk', 'ulysses'), may hold values from -6 to 6
- key_rows: bfloat16 [16, 1024, 1024], P('blk', 'ulysses'), may hold values from -6 to 6
- value_rows: bfloat16 [16, 1024, 1024], P('blk', 'ulysses'), may hold values from -6 to 6
- tile_segment: int32 [128], replicated, may hold values from 0 to 31, never falling along the last dimension, each value on 1 to 8 neighbouring positions
Outputs:
- attended: bfloat16 [16, 1024, 4096], P('blk', 'ulysses')
Inputs may be any that keep to these rules, and one draw needn't show every extreme that they name: `tile_segment`: segment numbers never fall along the sequence and each segment covers 1 to 8 tiles.
All inputs are finite; a program needn't handle non-finite values.
Results may differ from a plain program's by a relative error of at most 0.0045.
Values may be sent and summed in bfloat16 or wider, within the bound.
A program may use at most 64 MiB of HBM per device.

v0:
```python
import math
import jax
import jax.numpy as jnp
from jax import lax
from jax.sharding import PartitionSpec as P

HEAD_DIM = 128
TILE = 128
masked_score = -1e30


def side_by_side(arrays, axis, split_dim, concat_dim, along):
    widths = [a.shape[along] for a in arrays]
    both = jnp.concatenate(arrays, axis=along)
    whole = lax.all_to_all(both, axis, split_axis=split_dim, concat_axis=concat_dim, tiled=True)
    return tuple(jnp.split(whole, [sum(widths[:k]) for k in range(1, len(widths))], axis=along))


def partner_2(value, axis, bit):
    return lax.ppermute(value, axis, [(i, i ^ 1 << bit) for i in range(lax.axis_size(axis))])


def side_by_side_2(arrays, axis, dim, along):
    ends, at = ([], 0)
    for a in arrays[:-1]:
        at += a.shape[along]
        ends.append(at)
    both = jnp.concatenate(arrays, axis=along)
    return tuple(jnp.split(lax.all_gather(both, axis, axis=dim, tiled=True), ends, axis=along))


def segment_of(positions, tile_segment):
    tiles_total = tile_segment.shape[0]
    matches = (positions // TILE)[:, None] == jnp.arange(tiles_total, dtype=jnp.int32)[None, :]
    return jnp.sum(jnp.where(matches, tile_segment[None, :], 0), axis=1)


def visible(query_pos, query_seg, key_pos, key_seg):
    earlier = key_pos[None, :] <= query_pos[:, None]
    same_image = (key_seg[None, :] == query_seg[:, None]) & (query_seg[:, None] % 2 == 1)
    return earlier | same_image


def widen(source_rows, groups):
    tokens_dev = source_rows.shape[1]
    heads_here = source_rows.shape[2] // HEAD_DIM
    factor = max(1, groups // heads_here)
    spread = jnp.repeat(source_rows.reshape(1, tokens_dev, heads_here, HEAD_DIM), factor, axis=2)
    return spread.reshape(1, tokens_dev, heads_here * factor * HEAD_DIM)


def same_rows(row_ids):
    return row_ids


def update(current, allowed, query_block, key_block, value_block):
    maxima, denominators, weighted = current
    scores = jnp.einsum(
        "qkgd,skd->kgqs", query_block, key_block, preferred_element_type=jnp.float32
    )
    scores = jnp.where(allowed[None, None], scores * HEAD_DIM ** (-0.5), masked_score)
    new_max = jnp.maximum(maxima, jnp.max(scores, axis=3))
    weights = jnp.where(allowed[None, None], jnp.exp(scores - new_max[..., None]), 0.0)
    factor = jnp.exp(maxima - new_max)
    denominators = factor * denominators + jnp.sum(weights, axis=3)
    product = jnp.einsum(
        "kgqs,skd->kgqd",
        weights.astype(jnp.bfloat16),
        value_block,
        preferred_element_type=jnp.float32,
    )
    weighted = factor[..., None] * weighted + product
    return (new_max, denominators, weighted)


def keep_state(current, allowed, query_block, key_block, value_block):
    return current


def build_fold(query_rows, query_pos, tile_segment, key_position, kv_width):
    rows_total = query_rows.shape[0]
    kv_local = kv_width // HEAD_DIM
    group_size = query_rows.shape[1] // HEAD_DIM // kv_local
    shaped = query_rows.reshape(rows_total, kv_local, group_size, HEAD_DIM)
    query_seg = segment_of(query_pos, tile_segment)
    half_rows = rows_total // 2

    def fold_step(running, portion, offset):
        key_part, value_part = portion
        portion_rows = key_part.shape[0]
        block_rows = math.gcd(portion_rows, 512)
        block_total = portion_rows // block_rows
        key_blocks = key_part.reshape(block_total, block_rows, kv_local, HEAD_DIM)
        value_blocks = value_part.reshape(block_total, block_rows, kv_local, HEAD_DIM)

        def one_block(halves, inputs):
            key_block, value_block, block_number = inputs
            key_pos = key_position(
                block_number * block_rows + jnp.arange(block_rows, dtype=jnp.int32)
            )
            key_seg = segment_of(key_pos, tile_segment)
            results = []
            for half_index in range(2):
                row_low = half_index * half_rows
                row_high = row_low + half_rows
                allowed = visible(
                    query_pos[row_low:row_high], query_seg[row_low:row_high], key_pos, key_seg
                )
                results.append(
                    lax.cond(
                        jnp.any(allowed),
                        update,
                        keep_state,
                        halves[half_index],
                        allowed,
                        shaped[row_low:row_high],
                        key_block,
                        value_block,
                    )
                )
            return ((results[0], results[1]), None)

        running, unused = lax.scan(
            one_block, running, (key_blocks, value_blocks, jnp.arange(block_total, dtype=jnp.int32))
        )
        return running

    def empty_half():
        return (
            jnp.full((kv_local, group_size, half_rows), masked_score, jnp.float32),
            jnp.zeros((kv_local, group_size, half_rows), jnp.float32),
            jnp.zeros((kv_local, group_size, half_rows, HEAD_DIM), jnp.float32),
        )

    return (fold_step, (empty_half(), empty_half()))


def finish(running):
    outputs = [weighted / denominators[..., None] for maxima, denominators, weighted in running]
    joined = jnp.concatenate(outputs, axis=2)
    kv_local, group_size, rows_total, head_dim = joined.shape
    joined = jnp.transpose(joined, (2, 0, 1, 3)).reshape(
        rows_total, kv_local * group_size * head_dim
    )
    return joined.astype(jnp.bfloat16)


def local(queries, key_rows, value_rows, tile_segment):
    ulysses_count = lax.axis_size("ulysses")
    block_count = lax.axis_size("blk")
    tokens_dev = queries.shape[1]
    block_len = tokens_dev * ulysses_count
    block_index = lax.axis_index("blk")
    local_rows = jnp.arange(block_len, dtype=jnp.int32)
    moved = (
        lax.all_to_all(queries, "ulysses", split_axis=2, concat_axis=1, tiled=True),
        *side_by_side(
            (widen(key_rows, ulysses_count), widen(value_rows, ulysses_count)), "ulysses", 2, 1, 0
        ),
    )
    query_rows, key_local, value_local = (moved[0][0], moved[1][0], moved[2][0])
    half_rows = block_len // 2
    partner = block_count - 1 - block_index
    travelling = query_rows[half_rows:]
    for bit_index in range(block_count.bit_length() - 1):
        travelling = partner_2(travelling, "blk", bit_index)
    query_rows = jnp.concatenate([query_rows[:half_rows], travelling], axis=0)
    query_pos = jnp.concatenate(
        [
            block_index * block_len + local_rows[:half_rows],
            partner * block_len + local_rows[half_rows:],
        ]
    )
    fold_step, initial = build_fold(
        query_rows, query_pos, tile_segment, same_rows, key_local.shape[1]
    )
    running = fold_step(
        initial, side_by_side_2((key_local, value_local), "blk", 0, 1), jnp.int32(0)
    )
    out_rows = finish(running)
    returning = out_rows[half_rows:]
    for bit_index in range(block_count.bit_length() - 1):
        returning = partner_2(returning, "blk", bit_index)
    out_rows = jnp.concatenate([out_rows[:half_rows], returning], axis=0)
    attended = lax.all_to_all(out_rows[None], "ulysses", split_axis=1, concat_axis=2, tiled=True)
    return attended


def solution(mesh):
    return jax.shard_map(
        local,
        mesh=mesh,
        in_specs=(
            P("blk", "ulysses", None),
            P("blk", "ulysses", None),
            P("blk", "ulysses", None),
            P(),
        ),
        out_specs=P("blk", "ulysses", None),
        check_vma=False,
    )
```

profile of v0, /device:TPU:16, one launch (start us, length us, event | category | flops | bytes accessed | tf_op | source)
XLA Modules:
  0.0 428.8 jit_solution(16484188474409896511)
XLA Ops:
  10.6 29.6 %all_to_all.48 = bf16[16,2,8192]{2,1,0:T(2,128)(2,1)S(1)} all-to-all(bf16[16,2,8192]{2,1,0:T(2,128)(2,1)S(1)} %reshape.218), channel_id=1, replica_groups=mesh['ulysses'=16,'blk'=16] {'ulysses'}, dimensions={0} | all-to-all | bytes 1048576 | tf_op jit(solution)/shard_map/all_to_all | solution.py:15
  42.7 2.8 copy.75
  46.1 22.5 %reduce.4 = bf16[4096,64]{1,0:T(8,128)(2,1)S(1)} reduce(bf16[4096,1,64]{2,1,0:T(2,128)(2,1)S(1)} %bitcast.147, bf16[]{:T(256)} %broadcast.213), dimensions={1}, to_apply=%bitcast.127.reduce_sub_computation | reduce | bytes 1048578
  69.3 22.1 %all_to_all.49 = bf16[16,2,8192]{2,1,0:T(2,128)(2,1)S(1)} all-to-all(bf16[16,2,8192]{2,1,0:T(2,128)(2,1)S(1)} %reshape.220), channel_id=1, replica_groups=mesh['ulysses'=16,'blk'=16] {'ulysses'}, dimensions={0} | all-to-all | bytes 1048576 | tf_op jit(solution)/shard_map/all_to_all | solution.py:156
  92.6 2.3 copy.76
  95.3 1.5 collective-permute-done
  97.4 7.8 %collective-permute-done.1 = bf16[512,256]{1,0:T(8,128)(2,1)S(1)} collective-permute-done((bf16[512,256]{1,0:T(8,128)(2,1)S(1)}, bf16[512,256]{1,0:T(8,128)(2,1)S(1)}, u32[]{:S(2)}, u32[]{:S(2)}) %collective-permute-start.1) | collective-permute-done | bytes 262176 | tf_op jit(solution)/shard_map/ppermute | solution.py:20
  105.1 1.3 collective-permute-start.2
  106.5 6.1 %collective-permute-done.2 = bf16[512,256]{1,0:T(8,128)(2,1)S(1)} collective-permute-done((bf16[512,256]{1,0:T(8,128)(2,1)S(1)}, bf16[512,256]{1,0:T(8,128)(2,1)S(1)}, u32[]{:S(2)}, u32[]{:S(2)}) %collective-permute-start.2) | collective-permute-done | bytes 262176 | tf_op jit(solution)/shard_map/ppermute | solution.py:20
  113.5 7.3 %collective-permute-done.3 = bf16[512,256]{1,0:T(8,128)(2,1)S(1)} collective-permute-done((bf16[512,256]{1,0:T(8,128)(2,1)S(1)}, bf16[512,256]{1,0:T(8,128)(2,1)S(1)}, u32[]{:S(2)}, u32[]{:S(2)}) %collective-permute-start.3) | collective-permute-done | bytes 262176 | tf_op jit(solution)/shard_map/ppermute | solution.py:20
  121.9 5.7 %fusion.52 = (bf16[16384,128]{1,0:T(8,128)(2,1)}, bf16[16384,128]{1,0:T(8,128)(2,1)}) fusion(bf16[16384,256]{1,0:T(8,128)(2,1)} %all-gather.2.cloned.1.call-done), kind=kLoop, calls=%fused_computation.100 | loop fusion | bytes 16777216 | tf_op jit(solution)/shard_map/split | solution.py:29
  127.7 236.1 %while.23 = (s32[]{:T(128)}, f32[1,2,512]{2,1,0:T(2,128)S(1)}, f32[1,2,512]{2,1,0:T(2,128)S(1)}, f32[1,2,512,128]{3,2,1,0:T(8,128)S(1)}, f32[1,2,512]{2,1,0:T(2,...) while((s32[]{:T(128)}, f32[1,2,512]{2,1,0:T(2,128)S(1)}, ...), condition=%wide.region_13.14_spmd, body=%wide.region_1.13_spmd.sunk | while | flops 553869824 | bytes 18521024 | solution.py:123
  130.2 1.3 fusion.61
  132.8 2.2 conditional.5
  134.9 2.2 conditional.4
  139.6 1.3 fusion.61
  142.1 2.2 conditional.5
  144.3 2.2 conditional.4
  151.5 2.2 conditional.5
  153.7 2.2 conditional.4
  158.4 1.3 fusion.61
  160.9 2.2 conditional.5
  163.1 2.2 conditional.4
  170.3 2.2 conditional.5
  172.4 2.2 conditional.4
  177.1 1.3 fusion.61
  179.7 2.2 conditional.5
  181.8 2.2 conditional.4
  186.5 1.3 fusion.61
  189.0 2.2 conditional.5
  191.2 2.2 conditional.4
  198.4 2.2 conditional.5
  200.6 2.2 conditional.4
  205.3 1.3 fusion.61
  207.8 2.2 conditional.5
  210.0 2.2 conditional.4
  214.7 1.3 fusion.61
  217.2 2.2 conditional.5
  219.3 2.2 conditional.4
  226.6 2.2 conditional.5
  228.7 2.2 conditional.4
  233.4 1.3 fusion.61
  235.9 2.2 conditional.5
  238.1 2.2 conditional.4
  242.8 1.3 fusion.61
  245.3 2.2 conditional.5
  247.5 2.2 conditional.4
  252.2 1.3 fusion.61
  254.7 2.2 conditional.5
  256.9 2.2 conditional.4
  261.6 1.3 fusion.61
  264.1 2.2 conditional.5
  266.3 2.2 conditional.4
  273.5 2.2 conditional.5
  275.6 2.2 conditional.4
  282.9 2.2 conditional.4
  290.1 2.2 conditional.4
  364.6 1.5 collective-permute-done.4
  366.1 8.3 %collective-permute-done.5 = bf16[512,256]{0,1:T(8,128)(2,1)S(1)} collective-permute-done((bf16[512,256]{0,1:T(8,128)(2,1)S(1)}, bf16[512,256]{0,1:T(8,128)(2,1)S(1)}, u32[]{:S(2)}, u32[]{:S(2)}) %collective-permute-start.5) | collective-permute-done | bytes 262176 | tf_op jit(solution)/shard_map/ppermute | solution.py:20
  374.4 3.5 collective-permute-start.6
  377.9 5.7 %collective-permute-done.6 = bf16[512,256]{0,1:T(8,128)(2,1)S(1)} collective-permute-done((bf16[512,256]{0,1:T(8,128)(2,1)S(1)}, bf16[512,256]{0,1:T(8,128)(2,1)S(1)}, u32[]{:S(2)}, u32[]{:S(2)}) %collective-permute-start.6) | collective-permute-done | bytes 262176 | tf_op jit(solution)/shard_map/ppermute | solution.py:20
  384.4 7.7 %collective-permute-done.7 = bf16[512,256]{0,1:T(8,128)(2,1)S(1)} collective-permute-done((bf16[512,256]{0,1:T(8,128)(2,1)S(1)}, bf16[512,256]{0,1:T(8,128)(2,1)S(1)}, u32[]{:S(2)}, u32[]{:S(2)}) %collective-permute-start.7) | collective-permute-done | bytes 262176 | tf_op jit(solution)/shard_map/ppermute | solution.py:20
  393.0 3.9 reduce.5
  397.0 23.5 %all_to_all.50 = bf16[16,2,8192]{2,1,0:T(2,128)(2,1)S(1)} all-to-all(bf16[16,2,8192]{2,1,0:T(2,128)(2,1)S(1)} %reshape.222), channel_id=1, replica_groups=mesh['ulysses'=16,'blk'=16] {'ulysses'}, dimensions={0} | all-to-all | bytes 1048576 | tf_op jit(solution)/shard_map/all_to_all | solution.py:185
  (513 shorter events, 174.4 us)
Async XLA Ops:
  6.5 115.3 %all-gather.2.cloned.1.call-start = ((), (), s32[]{:S(2)}) async-start(), calls=%async_computation.3 | async-start | bytes 8912896 | tf_op jit(solution)/shard_map/all_gather | solution.py:29
  41.7 1.1 copy-start
  94.9 18.1 %copy-start.1 = (s32[128]{0:T(128)S(1)}, s32[128]{0:T(128)}, u32[]{:S(2)}) copy-start(s32[128]{0:T(128)} %param.13) | copy-start | bytes 1540
  95.2 1.6 collective-permute-start
  96.8 8.3 %collective-permute-start.1 = (bf16[512,256]{1,0:T(8,128)(2,1)S(1)}, bf16[512,256]{1,0:T(8,128)(2,1)S(1)}, u32[]{:S(2)}, u32[]{:S(2)}) collective-permute-start(bf16[512,256]{1,0:T(8,128)(2,1)S(1)} %collective-permute-done), channel_id=1, source_target_pairs={{0,2},{1,3},{2,0},{3,1},{4,6},{5,7},{6,4},{7,5},{8,10},{9,11},{10,... | collective-permute-start | bytes 786440 | tf_op jit(solution)/shard_map/ppermute | solution.py:20
  105.1 7.5 %collective-permute-start.2 = (bf16[512,256]{1,0:T(8,128)(2,1)S(1)}, bf16[512,256]{1,0:T(8,128)(2,1)S(1)}, u32[]{:S(2)}, u32[]{:S(2)}) collective-permute-start(bf16[512,256]{1,0:T(8,128)(2,1)S(1)} %collective-permute-done.1), channel_id=1, source_target_pairs={{0,4},{1,5},{2,6},{3,7},{4,0},{5,1},{6,2},{7,3},{8,12},{9,13},{10,... | collective-permute-start | bytes 786440 | tf_op jit(solution)/shard_map/ppermute | solution.py:20
  112.6 8.1 %collective-permute-start.3 = (bf16[512,256]{1,0:T(8,128)(2,1)S(1)}, bf16[512,256]{1,0:T(8,128)(2,1)S(1)}, u32[]{:S(2)}, u32[]{:S(2)}) collective-permute-start(bf16[512,256]{1,0:T(8,128)(2,1)S(1)} %collective-permute-done.2), channel_id=1, source_target_pairs={{0,8},{1,9},{2,10},{3,11},{4,12},{5,13},{6,14},{7,15},{8,0},{9,1},... | collective-permute-start | bytes 786440 | tf_op jit(solution)/shard_map/ppermute | solution.py:20
  364.5 1.6 collective-permute-start.4
  366.1 8.3 %collective-permute-start.5 = (bf16[512,256]{0,1:T(8,128)(2,1)S(1)}, bf16[512,256]{0,1:T(8,128)(2,1)S(1)}, u32[]{:S(2)}, u32[]{:S(2)}) collective-permute-start(bf16[512,256]{0,1:T(8,128)(2,1)S(1)} %collective-permute-done.4), channel_id=1, source_target_pairs={{0,2},{1,3},{2,0},{3,1},{4,6},{5,7},{6,4},{7,5},{8,10},{9,11},{10,... | collective-permute-start | bytes 786440 | tf_op jit(solution)/shard_map/ppermute | solution.py:20
  374.4 9.3 %collective-permute-start.6 = (bf16[512,256]{0,1:T(8,128)(2,1)S(1)}, bf16[512,256]{0,1:T(8,128)(2,1)S(1)}, u32[]{:S(2)}, u32[]{:S(2)}) collective-permute-start(bf16[512,256]{0,1:T(8,128)(2,1)S(1)} %collective-permute-done.5), channel_id=1, source_target_pairs={{0,4},{1,5},{2,6},{3,7},{4,0},{5,1},{6,2},{7,3},{8,12},{9,13},{10,... | collective-permute-start | bytes 786440 | tf_op jit(solution)/shard_map/ppermute | solution.py:20
  383.7 8.4 %collective-permute-start.7 = (bf16[512,256]{0,1:T(8,128)(2,1)S(1)}, bf16[512,256]{0,1:T(8,128)(2,1)S(1)}, u32[]{:S(2)}, u32[]{:S(2)}) collective-permute-start(bf16[512,256]{0,1:T(8,128)(2,1)S(1)} %collective-permute-done.6), channel_id=1, source_target_pairs={{0,8},{1,9},{2,10},{3,11},{4,12},{5,13},{6,14},{7,15},{8,0},{9,1},... | collective-permute-start | bytes 786440 | tf_op jit(solution)/shard_map/ppermute | solution.py:20
Sparse Core Ops, SparseCore 0:
  42.9 53.3 all-gather.1
where the time goes:
time: 431 us; the launch traced here: 429 us
  other arithmetic  99.3 us (23%)
  blocking collectives  75.2 us (17%)
  local copies, waits for them, and re-layouts  73.2 us (17%)
  loops' own time  63.6 us (15%)
  matrix products  50.9 us (12%)
  waiting for transfers between devices  46 us (11%)
  between operations  13.8 us (3%)
  starting transfers between devices  6.73 us (2%)
    another operation x1, loops' own time, fold_step(): lax.scan(one_block, running, (key_blocks, value_blocks, jnp.arange(block_...  61.4 us
    ppermute x8, waiting for transfers between devices, partner_2(): lax.ppermute(value, axis, [(i, i ^ 1 << bit) for i in range(lax.axis_size...  46 us
    reduce_or x32, other arithmetic, one_block(): jnp.any(allowed)  41.9 us
    dot_general x34, matrix products, update(): jnp.einsum('kgqs,skd->kgqd', weights.astype(jnp.bfloat16), value_block, p...  32.1 us
    squeeze x32, local copies, waits for them, and re-layouts, fold_step(): lax.scan(one_block, running, (key_blocks, value_blocks, jnp.arange(block_...  31.8 us
    all_to_all x1, blocking collectives, side_by_side(): lax.all_to_all(both, axis, split_axis=split_dim, concat_axis=concat_dim,...  29.6 us
    unnamed x2, other arithmetic  26.3 us
    all_to_all x1, blocking collectives, local(): lax.all_to_all(out_rows[None], 'ulysses', split_axis=1, concat_axis=2, ti...  23.5 us
  transfers between devices with their start and end apart: 9, of which 8 were waited for; matrix products, arithmetic and copies ran while one was open for 7% of the time, Pallas kernels for 0%

commit v1 on v0

--- a/solution.py
+++ b/solution.py
@@ -7,6 +7,11 @@
 HEAD_DIM = 128
 TILE = 128
 masked_score = -1e30
+
+
+def convert_the_sections(tile_in):
+    x_now = jnp.stack(jnp.split(tile_in, jax.lax.axis_size("ulysses"), 2), axis=0)
+    return jnp.concatenate(jax.lax.all_to_all(x_now, "ulysses", 0, 0), 1)
 
 
 def side_by_side(arrays, axis, split_dim, concat_dim, along):
@@ -153,7 +158,7 @@
     block_index = lax.axis_index("blk")
     local_rows = jnp.arange(block_len, dtype=jnp.int32)
     moved = (
-        lax.all_to_all(queries, "ulysses", split_axis=2, concat_axis=1, tiled=True),
+        convert_the_sections(queries),
         *side_by_side(
             (widen(key_rows, ulysses_count), widen(value_rows, ulysses_count)), "ulysses", 2, 1, 0
         ),

time: 431 us -> 420 us (0.974)
  other arithmetic: 99.3 us -> 76.6 us
  waiting for transfers between devices: 46 us -> 60.7 us
  local copies, waits for them, and re-layouts: 73.2 us -> 65.8 us
    unnamed x2 -> x1, other arithmetic: 26.3 us -> 3.82 us
    ppermute x8, waiting for transfers between devices: 46 us -> 59.4 us  [partner_2(): lax.ppermute(value, axis, [(i, i ^ 1 << bit) for i in range(lax.axis_size...]
    unnamed x16 -> x27, local copies, waits for them, and re-layouts: 9.37 us -> 4.57 us
  transfers between devices with their start and end apart: 9 -> 9, of which waited for: 8 -> 9; matrix products, arithmetic and copies ran while one was open for 7% -> 0% of each run, Pallas kernels for 0% -> 0%
where the time goes in v1:
time: 420 us; the launch traced here: 418 us
  blocking collectives  77.2 us (18%)
  other arithmetic  76.6 us (18%)
  local copies, waits for them, and re-layouts  65.8 us (16%)
  loops' own time  63.3 us (15%)
  waiting for transfers between devices  60.7 us (14%)
  matrix products  51.1 us (12%)
  between operations  13.9 us (3%)
  starting transfers between devices  9.37 us (2%)
    another operation x1, loops' own time, fold_step(): lax.scan(one_block, running, (key_blocks, value_blocks, jnp.arange(block_...  61.4 us
    ppermute x8, waiting for transfers between devices, partner_2(): lax.ppermute(value, axis, [(i, i ^ 1 << bit) for i in range(lax.axis_size...  59.4 us
    reduce_or x32, other arithmetic, one_block(): jnp.any(allowed)  41.9 us
    dot_general x34, matrix products, update(): jnp.einsum('kgqs,skd->kgqd', weights.astype(jnp.bfloat16), value_block, p...  32.3 us
    squeeze x32, local copies, waits for them, and re-layouts, fold_step(): lax.scan(one_block, running, (key_blocks, value_blocks, jnp.arange(block_...  31.5 us
    all_to_all x1, blocking collectives, side_by_side(): lax.all_to_all(both, axis, split_axis=split_dim, concat_axis=concat_dim,...  29.6 us
    all_to_all x1, blocking collectives, local(): lax.all_to_all(out_rows[None], 'ulysses', split_axis=1, concat_axis=2, ti...  25.5 us
    all_to_all x1, blocking collectives, convert_the_sections(): return jnp.concatenate(jax.lax.all_to_all(x_now, 'ulysses', 0, 0), 1)  22.1 us
  transfers between devices with their start and end apart: 9, of which 9 were waited for; matrix products, arithmetic and copies ran while one was open for 0% of the time, Pallas kernels for 0%

profile of v1, /device:TPU:16, one launch (start us, length us, event | category | flops | bytes accessed | tf_op | source)
XLA Modules:
  0.0 418.0 jit_solution(6411658175752980964)
XLA Ops:
  10.6 29.6 %all_to_all.38 = bf16[16,2,8192]{2,1,0:T(2,128)(2,1)S(1)} all-to-all(bf16[16,2,8192]{2,1,0:T(2,128)(2,1)S(1)} %reshape.217), channel_id=1, replica_groups=mesh['ulysses'=16,'blk'=16] {'ulysses'}, dimensions={0} | all-to-all | bytes 1048576 | tf_op jit(solution)/shard_map/all_to_all | solution.py:20
  43.0 22.1 %all_to_all.39 = bf16[16,1,64,256]{3,2,1,0:T(8,128)(2,1)S(1)} all-to-all(bf16[16,1,64,256]{3,2,1,0:T(8,128)(2,1)S(1)} %constant_dynamic-update-slice_fusion), channel_id=1, replica_groups=mesh['ulysses'=16,'blk'=16] {'ulysses'}, dimensions={0} | all-to-all | bytes 1048576 | tf_op jit(solution)/shard_map/all_to_all | solution.py:14
  65.2 1.5 collective-permute-done
  67.3 7.8 %collective-permute-done.1 = bf16[512,256]{1,0:T(8,128)(2,1)S(1)} collective-permute-done((bf16[512,256]{1,0:T(8,128)(2,1)S(1)}, bf16[512,256]{1,0:T(8,128)(2,1)S(1)}, u32[]{:S(2)}, u32[]{:S(2)}) %collective-permute-start.1) | collective-permute-done | bytes 262176 | tf_op jit(solution)/shard_map/ppermute | solution.py:25
  75.1 7.7 %collective-permute-start.2 = (bf16[512,256]{1,0:T(8,128)(2,1)S(1)}, bf16[512,256]{1,0:T(8,128)(2,1)S(1)}, u32[]{:S(2)}, u32[]{:S(2)}) collective-permute-start(bf16[512,256]{1,0:T(8,128)(2,1)S(1)} %collective-permute-done.1), channel_id=1, source_target_pairs={{0,4},{1,5},{2,6},{3,7},{4,0},{5,1},{6,2},{7,3},{8,12},{9,13},{10,... | collective-permute-start | bytes 786440 | tf_op jit(solution)/shard_map/ppermute | solution.py:25
  82.8 11.9 %collective-permute-done.2 = bf16[512,256]{1,0:T(8,128)(2,1)S(1)} collective-permute-done((bf16[512,256]{1,0:T(8,128)(2,1)S(1)}, bf16[512,256]{1,0:T(8,128)(2,1)S(1)}, u32[]{:S(2)}, u32[]{:S(2)}) %collective-permute-start.2) | collective-permute-done | bytes 262176 | tf_op jit(solution)/shard_map/ppermute | solution.py:25
  95.1 13.6 %collective-permute-done.3 = bf16[512,256]{1,0:T(8,128)(2,1)S(1)} collective-permute-done((bf16[512,256]{1,0:T(8,128)(2,1)S(1)}, bf16[512,256]{1,0:T(8,128)(2,1)S(1)}, u32[]{:S(2)}, u32[]{:S(2)}) %collective-permute-start.3) | collective-permute-done | bytes 262176 | tf_op jit(solution)/shard_map/ppermute | solution.py:25
  111.1 5.7 %fusion.52 = (bf16[16384,128]{1,0:T(8,128)(2,1)}, bf16[16384,128]{1,0:T(8,128)(2,1)}) fusion(bf16[16384,256]{1,0:T(8,128)(2,1)} %all-gather.2.cloned.1.call-done), kind=kLoop, calls=%fused_computation.115 | loop fusion | bytes 16777216 | tf_op jit(solution)/shard_map/split | solution.py:34
  116.9 235.6 %while.23 = (s32[]{:T(128)}, f32[1,2,512]{2,1,0:T(2,128)S(1)}, f32[1,2,512]{2,1,0:T(2,128)S(1)}, f32[1,2,512,128]{3,2,1,0:T(8,128)S(1)}, f32[1,2,512]{2,1,0:T(2,...) while((s32[]{:T(128)}, f32[1,2,512]{2,1,0:T(2,128)S(1)}, ...), condition=%wide.region_13.14_spmd, body=%wide.region_1.13_spmd.sunk | while | flops 553869824 | bytes 18521016 | solution.py:128
  118.5 1.3 fusion.60
  121.4 2.2 conditional.5
  124.1 2.2 conditional.4
  127.8 1.3 fusion.60
  130.8 2.2 conditional.5
  133.5 2.2 conditional.4
  137.2 1.3 fusion.60
  140.2 2.2 conditional.5
  142.9 2.2 conditional.4
  146.6 1.3 fusion.60
  149.5 2.2 conditional.5
  152.2 2.2 conditional.4
  155.9 1.3 fusion.60
  158.9 2.2 conditional.5
  161.6 2.2 conditional.4
  165.3 1.3 fusion.60
  168.2 2.2 conditional.5
  171.0 2.2 conditional.4
  174.7 1.3 fusion.60
  177.6 2.2 conditional.5
  180.3 2.2 conditional.4
  184.0 1.3 fusion.60
  187.0 2.2 conditional.5
  189.7 2.2 conditional.4
  196.3 2.2 conditional.5
  199.1 2.2 conditional.4
  202.8 1.3 fusion.60
  205.7 2.2 conditional.5
  208.4 2.2 conditional.4
  215.1 2.2 conditional.5
  217.8 2.2 conditional.4
  221.5 1.3 fusion.60
  224.4 2.2 conditional.5
  227.1 2.2 conditional.4
  233.8 2.2 conditional.5
  236.5 2.2 conditional.4
  240.2 1.3 fusion.60
  243.2 2.2 conditional.5
  245.9 2.2 conditional.4
  252.5 2.2 conditional.5
  255.2 2.2 conditional.4
  258.9 1.3 fusion.60
  261.9 2.2 conditional.5
  264.6 2.2 conditional.4
  271.8 2.2 conditional.4
  275.5 1.3 fusion.60
  279.1 2.2 conditional.4
  282.8 1.3 fusion.60
  292.9 1.3 fusion.60
  353.2 1.5 collective-permute-done.4
  354.8 8.3 %collective-permute-done.5 = bf16[512,256]{0,1:T(8,128)(2,1)S(1)} collective-permute-done((bf16[512,256]{0,1:T(8,128)(2,1)S(1)}, bf16[512,256]{0,1:T(8,128)(2,1)S(1)}, u32[]{:S(2)}, u32[]{:S(2)}) %collective-permute-start.5) | collective-permute-done | bytes 262176 | tf_op jit(solution)/shard_map/ppermute | solution.py:25
  363.3 7.3 %collective-permute-done.6 = bf16[512,256]{0,1:T(8,128)(2,1)S(1)} collective-permute-done((bf16[512,256]{0,1:T(8,128)(2,1)S(1)}, bf16[512,256]{0,1:T(8,128)(2,1)S(1)}, u32[]{:S(2)}, u32[]{:S(2)}) %collective-permute-start.6) | collective-permute-done | bytes 262176 | tf_op jit(solution)/shard_map/ppermute | solution.py:25
  371.3 7.4 %collective-permute-done.7 = bf16[512,256]{0,1:T(8,128)(2,1)S(1)} collective-permute-done((bf16[512,256]{0,1:T(8,128)(2,1)S(1)}, bf16[512,256]{0,1:T(8,128)(2,1)S(1)}, u32[]{:S(2)}, u32[]{:S(2)}) %collective-permute-start.7) | collective-permute-done | bytes 262176 | tf_op jit(solution)/shard_map/ppermute | solution.py:25
  380.2 3.8 reduce.4
  384.1 25.5 %all_to_all.40 = bf16[16,2,8192]{2,1,0:T(2,128)(2,1)S(1)} all-to-all(bf16[16,2,8192]{2,1,0:T(2,128)(2,1)S(1)} %reshape.219), channel_id=1, replica_groups=mesh['ulysses'=16,'blk'=16] {'ulysses'}, dimensions={0} | all-to-all | bytes 1048576 | tf_op jit(solution)/shard_map/all_to_all | solution.py:190
  (521 shorter events, 167.8 us)
Async XLA Ops:
  6.5 104.6 %all-gather.2.cloned.1.call-start = ((), (), s32[]{:S(2)}) async-start(), calls=%async_computation.3 | async-start | bytes 8912896 | tf_op jit(solution)/shard_map/all_gather | solution.py:34
  41.7 1.1 copy-start
  41.9 52.8 %copy-start.1 = (s32[128]{0:T(128)S(1)}, s32[128]{0:T(128)}, u32[]{:S(2)}) copy-start(s32[128]{0:T(128)} %param.13) | copy-start | bytes 1540
  65.1 1.6 collective-permute-start
  66.7 8.3 %collective-permute-start.1 = (bf16[512,256]{1,0:T(8,128)(2,1)S(1)}, bf16[512,256]{1,0:T(8,128)(2,1)S(1)}, u32[]{:S(2)}, u32[]{:S(2)}) collective-permute-start(bf16[512,256]{1,0:T(8,128)(2,1)S(1)} %collective-permute-done), channel_id=1, source_target_pairs={{0,2},{1,3},{2,0},{3,1},{4,6},{5,7},{6,4},{7,5},{8,10},{9,11},{10,... | collective-permute-start | bytes 786440 | tf_op jit(solution)/shard_map/ppermute | solution.py:25
  75.1 19.6 %collective-permute-start.2 = (bf16[512,256]{1,0:T(8,128)(2,1)S(1)}, bf16[512,256]{1,0:T(8,128)(2,1)S(1)}, u32[]{:S(2)}, u32[]{:S(2)}) collective-permute-start(bf16[512,256]{1,0:T(8,128)(2,1)S(1)} %collective-permute-done.1), channel_id=1, source_target_pairs={{0,4},{1,5},{2,6},{3,7},{4,0},{5,1},{6,2},{7,3},{8,12},{9,13},{10,... | collective-permute-start | bytes 786440 | tf_op jit(solution)/shard_map/ppermute | solution.py:25
  94.6 14.1 %collective-permute-start.3 = (bf16[512,256]{1,0:T(8,128)(2,1)S(1)}, bf16[512,256]{1,0:T(8,128)(2,1)S(1)}, u32[]{:S(2)}, u32[]{:S(2)}) collective-permute-start(bf16[512,256]{1,0:T(8,128)(2,1)S(1)} %collective-permute-done.2), channel_id=1, source_target_pairs={{0,8},{1,9},{2,10},{3,11},{4,12},{5,13},{6,14},{7,15},{8,0},{9,1},... | collective-permute-start | bytes 786440 | tf_op jit(solution)/shard_map/ppermute | solution.py:25
  353.1 1.6 collective-permute-start.4
  354.8 8.3 %collective-permute-start.5 = (bf16[512,256]{0,1:T(8,128)(2,1)S(1)}, bf16[512,256]{0,1:T(8,128)(2,1)S(1)}, u32[]{:S(2)}, u32[]{:S(2)}) collective-permute-start(bf16[512,256]{0,1:T(8,128)(2,1)S(1)} %collective-permute-done.4), channel_id=1, source_target_pairs={{0,2},{1,3},{2,0},{3,1},{4,6},{5,7},{6,4},{7,5},{8,10},{9,11},{10,... | collective-permute-start | bytes 786440 | tf_op jit(solution)/shard_map/ppermute | solution.py:25
  363.1 7.5 %collective-permute-start.6 = (bf16[512,256]{0,1:T(8,128)(2,1)S(1)}, bf16[512,256]{0,1:T(8,128)(2,1)S(1)}, u32[]{:S(2)}, u32[]{:S(2)}) collective-permute-start(bf16[512,256]{0,1:T(8,128)(2,1)S(1)} %collective-permute-done.5), channel_id=1, source_target_pairs={{0,4},{1,5},{2,6},{3,7},{4,0},{5,1},{6,2},{7,3},{8,12},{9,13},{10,... | collective-permute-start | bytes 786440 | tf_op jit(solution)/shard_map/ppermute | solution.py:25
  370.6 8.1 %collective-permute-start.7 = (bf16[512,256]{0,1:T(8,128)(2,1)S(1)}, bf16[512,256]{0,1:T(8,128)(2,1)S(1)}, u32[]{:S(2)}, u32[]{:S(2)}) collective-permute-start(bf16[512,256]{0,1:T(8,128)(2,1)S(1)} %collective-permute-done.6), channel_id=1, source_target_pairs={{0,8},{1,9},{2,10},{3,11},{4,12},{5,13},{6,14},{7,15},{8,0},{9,1},... | collective-permute-start | bytes 786440 | tf_op jit(solution)/shard_map/ppermute | solution.py:25
Sparse Core Ops, SparseCore 0:
  42.9 68.1 all-gather.1
